TPU v7x, 256 devices: a whole 4x4x8 slice. The times are simulated.
256 devices in a mesh: view: 8 (over x, core), gauss: 32 (over y, z).
Axes of the slice: x: 4, y: 4, z: 8, core: 2. Of those that a mesh axis runs over, the one named last changes fastest.
Arguments:
- means: float32 [3, 524288], P(None, 'gauss'), may hold values from -1 to 1
- scales: float32 [3, 524288], P(None, 'gauss'), may hold values from 0.05 to 0.6
- quats: float32 [4, 524288], P(None, 'gauss'), may hold values from -6 to 6
- attrs: float32 [49, 524288], P(None, 'gauss'), may hold values from -6 to 6
- grad_screen: float32 [32, 2, 524288], P('view', None, 'gauss'), may hold values from -6 to 6
- visible: int32 [32, 524288], P('view', 'gauss'), may hold values 0 or 1
- clone_mask: int32 [524288], P('gauss'), may hold values from 0 to 1, as said below
- rotation: float32 [32, 3, 3], P('view'), may hold values from -3.5 to 3.5
- shift: float32 [32, 3], P('view'), may hold values from 2 to 5
- focal: float32 [32], P('view'), may hold values from 1 to 4
Outputs:
- peak_stats: float32 [2, 524288], P(None, 'gauss')
- clones: float32 [61, 524288], P(None, 'gauss')
- clone_total: int32 [], replicated
Inputs may be any that keep to these rules, and one draw needn't show every extreme that they name: `clone_mask`: in every draw some shard of 16384 consecutive Gaussians has all of them marked.
All inputs are finite; a program needn't handle non-finite values. No bound on the sum of `visible` on one device may be relied on, other than what follows from the above.
Results may differ from a plain program's by a relative error of at most 0.0003.
Values sent between devices are 32-bit elements; how exact they have to be, the bound alone decides.
No kernel may reach another device: no remote copies, remote signals or barrier semaphores. Data moves between devices by JAX's collectives and lax.ppermute only.
A program may use at most 128 MiB of HBM per device.

v0:
```python
import jax
import jax.numpy as jnp
from jax import lax
from jax.sharding import PartitionSpec as P

G_DEV = 16384


def copy_for_each(x, axis):
    count = lax.axis_size(axis)
    return lax.all_to_all(jnp.broadcast_to(x[None], (count, *x.shape)), axis, 0, 0, tiled=True)


def of_everyone(x, axis):
    return copy_for_each(x, axis).max(axis=0)


def together(arrays, axis):
    vector, at, done = (jnp.concatenate([a.reshape(-1) for a in arrays]), 0, [])
    running = of_everyone(vector, axis)
    for a in arrays:
        done.append(running[at : at + a.size].reshape(a.shape))
        at += a.size
    return tuple(done)


def folded_in_pairs(pieces, combine):
    while len(jax.tree.leaves(pieces)[0]) > 1:
        pieces = jax.vmap(combine)(*(pieces[side::2] for side in (0, 1)))
    return pieces[0]


def prefix(x, axis, combine, identity):
    count, mine = (lax.axis_size(axis), lax.axis_index(axis))
    passed = jnp.arange(count) < mine

    def kept(part, zero, own):
        part = jnp.where(
            passed.reshape(-1, *(1 for _ in own.shape)), part, jnp.asarray(zero, own.dtype)
        )
        return part

    pieces = copy_for_each(x, axis)
    return folded_in_pairs(kept(pieces, identity, x), combine)


def of_everyone_2(x, axis):
    everything = copy_for_each(x, axis)
    return jnp.sum(everything, axis=0)


def quat_factor(scales, quats):
    inv = 1.0 / jnp.sqrt(jnp.sum(quats * quats, axis=0) + 0.25)
    w, x, y, z = (quats[0] * inv, quats[1] * inv, quats[2] * inv, quats[3] * inv)
    rq = [
        [1 - 2 * (y * y + z * z), 2 * (x * y - w * z), 2 * (x * z + w * y)],
        [2 * (x * y + w * z), 1 - 2 * (x * x + z * z), 2 * (y * z - w * x)],
        [2 * (x * z - w * y), 2 * (y * z + w * x), 1 - 2 * (x * x + y * y)],
    ]
    return [[rq[i][j] * scales[j] for j in range(3)] for i in range(3)]


def view_stats(means, factor, grad, seen, rot, trans, focal_v):
    point = [
        rot[i, 0] * means[0] + rot[i, 1] * means[1] + rot[i, 2] * means[2] + trans[i]
        for i in range(3)
    ]
    depth = jnp.maximum(point[2], 1.0)
    j00 = focal_v / depth
    j02 = -focal_v * point[0] / (depth * depth)
    j12 = -focal_v * point[1] / (depth * depth)
    first = [j00 * rot[0, j] + j02 * rot[2, j] for j in range(3)]
    second = [j00 * rot[1, j] + j12 * rot[2, j] for j in range(3)]
    prow = [sum((first[j] * factor[j][k] for j in range(3))) for k in range(3)]
    qrow = [sum((second[j] * factor[j][k] for j in range(3))) for k in range(3)]
    a_val = prow[0] ** 2 + prow[1] ** 2 + prow[2] ** 2 + 0.3
    c_val = qrow[0] ** 2 + qrow[1] ** 2 + qrow[2] ** 2 + 0.3
    b_val = prow[0] * qrow[0] + prow[1] * qrow[1] + prow[2] * qrow[2]
    half = 0.5 * (a_val - c_val)
    lam = 0.5 * (a_val + c_val) + jnp.sqrt(half * half + b_val * b_val + 0.01)
    seenf = seen.astype(jnp.float32)
    radius = 3.0 * jnp.sqrt(lam) * seenf
    gnorm = jnp.sqrt(grad[0] * grad[0] + grad[1] * grad[1]) * seenf
    return (gnorm, radius)


def add_ints(earlier, later):
    return earlier + later


def body(means, scales, quats, attrs, grad_screen, visible, clone_mask, rotation, shift, focal):
    factor = quat_factor(scales, quats)
    gmax = jnp.zeros(means.shape[1], jnp.float32)
    rmax = jnp.zeros(means.shape[1], jnp.float32)
    for v in range(grad_screen.shape[0]):
        gnorm, radius = view_stats(
            means, factor, grad_screen[v], visible[v], rotation[v], shift[v], focal[v]
        )
        gmax = jnp.maximum(gmax, gnorm)
        rmax = jnp.maximum(rmax, radius)
    gmax, rmax = together((gmax, rmax), "view")
    peak = jnp.stack([gmax, rmax])
    rows = jnp.concatenate([means, scales, quats, attrs, peak], axis=0)
    feat_rows = rows.shape[0]
    shards = lax.axis_size("gauss")
    cap_blk = G_DEV // 128
    count = jnp.sum(clone_mask)
    blocks = (count + 127) // 128
    offset = prefix(blocks, "gauss", add_ints, jnp.int32(0))
    summed = of_everyone_2(count.astype(jnp.float32), "gauss")
    total = summed.astype(jnp.int32)
    rank = jnp.cumsum(clone_mask) - 1
    where_to = jnp.where(clone_mask == 1, rank, cap_blk * 128)
    packed = (
        jnp.zeros((feat_rows, cap_blk * 128), jnp.float32).at[:, where_to].set(rows, mode="drop")
    )
    packed = packed.reshape(feat_rows, cap_blk, 128)
    per = (cap_blk + shards - 1) // shards
    target = jnp.arange(shards, dtype=jnp.int32)[:, None]
    within = jnp.arange(per, dtype=jnp.int32)[None, :]
    local_blk = (target - offset) % shards + within * shards
    valid = local_blk < blocks
    picked = jnp.minimum(local_blk, cap_blk - 1).reshape(-1)
    outgoing = packed[:, picked, :] * valid.reshape(1, -1, 1).astype(jnp.float32)
    outgoing = outgoing.reshape(feat_rows, shards, per, 128)
    slot_ids = (
        jnp.where(valid, (offset + local_blk) // shards, cap_blk)
        .astype(jnp.int32)
        .reshape(1, shards, per)
    )
    width = 128 // lax.axis_size("view")
    start = lax.axis_index("view") * width
    portion = lax.dynamic_slice_in_dim(outgoing, start, width, 3)
    arrived, slots_in = (
        lax.all_to_all(portion, "gauss", split_axis=1, concat_axis=1, tiled=True),
        lax.all_to_all(slot_ids, "gauss", split_axis=1, concat_axis=1, tiled=True),
    )
    arrived = arrived.reshape(feat_rows, shards * per, width)
    partial_place = (
        jnp.zeros((feat_rows, cap_blk, width), jnp.float32)
        .at[:, slots_in.reshape(-1)]
        .set(arrived, mode="drop")
    )
    placed = lax.all_gather(partial_place, "view", axis=2, tiled=True)
    clones = placed.reshape(feat_rows, cap_blk * 128)
    return (peak, clones, total)


def solution(mesh):
    return jax.shard_map(
        body,
        mesh=mesh,
        in_specs=(
            P(None, "gauss"),
            P(None, "gauss"),
            P(None, "gauss"),
            P(None, "gauss"),
            P("view", None, "gauss"),
            P("view", "gauss"),
            P("gauss"),
            P("view", None, None),
            P("view", None),
            P("view"),
        ),
        out_specs=(P(None, "gauss"), P(None, "gauss"), P()),
        check_vma=False,
    )
```

profile of v0, /device:TPU:1, one launch (start us, length us, event | category | flops | bytes accessed | tf_op | source)
XLA Modules:
  0.0 326.7 jit_solution(10295088173397887772)
XLA Ops:
  12.2 12.0 %all-to-all-start.1 = ((s32[32,1,1]{2,1,0:T(1,128)}), s32[32,1,1]{2,1,0:T(1,128)S(1)}, u32[]{:S(2)}, u32[]{:S(2)}) async-start(s32[32,1,1]{2,1,0:T(1,128)} %broadcast_in_dim.45), calls=%async_computation.1 | async-start | bytes 32768 | tf_op jit(solution)/shard_map/all_to_all | solution.py:11
  33.8 7.2 %multiply_add_fusion.23 = (f32[1,16384]{1,0:T(1,128)S(1)}, f32[1,16384]{1,0:T(1,128)S(1)}, f32[1,16384]{1,0:T(1,128)S(1)}, f32[1,16384]{1,0:T(1,128)S(1)}) fusion(f32[]{:T(128)} %bitcast.13, f32[]{:T(128)} %bitcast.9, f32[]{:T(128)} %bitcast.16, f32[3,16384]{1,0:T(4,128)} %param.10, f32[]{:T(128)} %bitcast.15, f32[]{:T(128)} %bitcast.14, f32[]{:T(128)S(6)} %neg.16, ...), kind=kLoop, calls=%fused_computation.35 | loop fusion | flops 327680 | bytes 458792 | tf_op jit(solution)/shard_map/add | solution.py:72
  41.1 7.3 %multiply_add_fusion.22 = (f32[1,16384]{1,0:T(1,128)S(1)}, f32[1,16384]{1,0:T(1,128)S(1)}, f32[1,16384]{1,0:T(1,128)S(1)}, f32[1,16384]{1,0:T(1,128)S(1)}) fusion(f32[1,16384]{1,0:T(1,128)S(1)} %get-tuple-element.22, f32[1,16384]{1,0:T(1,128)S(1)} %get-tuple-element.23, f32[]{:T(128)} %bitcast.14, f32[]{:T(128)} %bitcast.10, f32[]{:T(128)} %bitcast.11, ...), kind=kLoop, calls=%fused_computation.34 | loop fusion | flops 294912 | bytes 655400 | tf_op jit(solution)/shard_map/add | solution.py:72
  52.2 7.4 %multiply_add_fusion.17 = (f32[1,16384]{1,0:T(1,128)S(1)}, f32[1,16384]{1,0:T(1,128)S(1)}, f32[1,16384]{1,0:T(1,128)S(1)}, f32[1,16384]{1,0:T(1,128)S(1)}) fusion(f32[]{:T(128)} %bitcast.39, f32[]{:T(128)} %bitcast.35, f32[]{:T(128)} %bitcast.42, f32[3,16384]{1,0:T(4,128)} %param.10, f32[]{:T(128)} %bitcast.41, f32[]{:T(128)} %bitcast.40, f32[]{:T(128)S(6)} %neg.17, ...), kind=kLoop, calls=%fused_computation.29 | loop fusion | flops 327680 | bytes 458792 | tf_op jit(solution)/shard_map/add | solution.py:72
  59.6 7.2 %multiply_add_fusion.16 = (f32[1,16384]{1,0:T(1,128)S(1)}, f32[1,16384]{1,0:T(1,128)S(1)}, f32[1,16384]{1,0:T(1,128)S(1)}, f32[1,16384]{1,0:T(1,128)S(1)}) fusion(f32[1,16384]{1,0:T(1,128)S(1)} %get-tuple-element.28, f32[1,16384]{1,0:T(1,128)S(1)} %get-tuple-element.29, f32[]{:T(128)} %bitcast.40, f32[]{:T(128)} %bitcast.36, f32[]{:T(128)} %bitcast.37, ...), kind=kLoop, calls=%fused_computation.28 | loop fusion | flops 294912 | bytes 655400 | tf_op jit(solution)/shard_map/add | solution.py:72
  70.7 7.4 %multiply_add_fusion.11 = (f32[1,16384]{1,0:T(1,128)S(1)}, f32[1,16384]{1,0:T(1,128)S(1)}, f32[1,16384]{1,0:T(1,128)S(1)}, f32[1,16384]{1,0:T(1,128)S(1)}) fusion(f32[]{:T(128)} %bitcast.58, f32[]{:T(128)} %bitcast.54, f32[]{:T(128)} %bitcast.61, f32[3,16384]{1,0:T(4,128)} %param.10, f32[]{:T(128)} %bitcast.60, f32[]{:T(128)} %bitcast.59, f32[]{:T(128)S(6)} %neg.18, ...), kind=kLoop, calls=%fused_computation.23 | loop fusion | flops 327680 | bytes 458792 | tf_op jit(solution)/shard_map/add | solution.py:72
  78.1 7.4 %multiply_add_fusion.10 = (f32[1,16384]{1,0:T(1,128)S(1)}, f32[1,16384]{1,0:T(1,128)S(1)}, f32[1,16384]{1,0:T(1,128)S(1)}, f32[1,16384]{1,0:T(1,128)S(1)}) fusion(f32[1,16384]{1,0:T(1,128)S(1)} %get-tuple-element.34, f32[1,16384]{1,0:T(1,128)S(1)} %get-tuple-element.35, f32[]{:T(128)} %bitcast.59, f32[]{:T(128)} %bitcast.55, f32[]{:T(128)} %bitcast.56, ...), kind=kLoop, calls=%fused_computation.22 | loop fusion | flops 294912 | bytes 655400 | tf_op jit(solution)/shard_map/add | solution.py:72
  85.4 2.6 multiply_add_fusion.7
  89.4 7.4 %multiply_add_fusion.5 = (f32[1,16384]{1,0:T(1,128)S(1)}, f32[1,16384]{1,0:T(1,128)S(1)}, f32[1,16384]{1,0:T(1,128)S(1)}, f32[1,16384]{1,0:T(1,128)S(1)}) fusion(f32[]{:T(128)} %bitcast.77, f32[]{:T(128)} %bitcast.73, f32[]{:T(128)} %bitcast.80, f32[3,16384]{1,0:T(4,128)} %param.10, f32[]{:T(128)} %bitcast.79, f32[]{:T(128)} %bitcast.78, f32[]{:T(128)S(6)} %neg.19, ...), kind=kLoop, calls=%fused_computation.17 | loop fusion | flops 327680 | bytes 458792 | tf_op jit(solution)/shard_map/add | solution.py:72
  96.8 7.4 %multiply_add_fusion.4 = (f32[1,16384]{1,0:T(1,128)S(1)}, f32[1,16384]{1,0:T(1,128)S(1)}, f32[1,16384]{1,0:T(1,128)S(1)}, f32[1,16384]{1,0:T(1,128)S(1)}) fusion(f32[1,16384]{1,0:T(1,128)S(1)} %get-tuple-element.40, f32[1,16384]{1,0:T(1,128)S(1)} %get-tuple-element.41, f32[]{:T(128)} %bitcast.78, f32[]{:T(128)} %bitcast.74, f32[]{:T(128)} %bitcast.75, ...), kind=kLoop, calls=%fused_computation.16 | loop fusion | flops 294912 | bytes 655400 | tf_op jit(solution)/shard_map/add | solution.py:72
  104.2 2.6 multiply_add_fusion.1
  113.5 5.3 %all-to-all-start = ((f32[8,1,32768]{2,1,0:T(1,128)}), f32[8,1,32768]{2,1,0:T(1,128)S(1)}, u32[]{:S(2)}, u32[]{:S(2)}) async-start(f32[8,1,32768]{2,1,0:T(1,128)} %broadcast_in_dim.24), calls=%async_computation | async-start | bytes 2097152 | tf_op jit(solution)/shard_map/all_to_all | solution.py:11
  125.2 8.5 %all-to-all-done = f32[8,1,32768]{2,1,0:T(1,128)S(1)} async-done(((f32[8,1,32768]{2,1,0:T(1,128)}), f32[8,1,32768]{2,1,0:T(1,128)S(1)}, u32[]{:S(2)}, u32[]{:S(2)}) %all-to-all-start) | async-done | bytes 1048608 | tf_op jit(solution)/shard_map/all_to_all | solution.py:11
  133.7 9.7 %all-to-all-start.2 = ((s32[1,32,4]{2,0,1:T(1,128)}), s32[1,32,4]{2,0,1:T(1,128)S(1)}, u32[]{:S(2)}, u32[]{:S(2)}) async-start(s32[1,32,4]{2,0,1:T(1,128)} %compare_select_fusion.1), calls=%async_computation.2 | async-start | bytes 32768 | tf_op jit(solution)/shard_map/all_to_all | solution.py:136
  144.2 21.5 %concatenate.8 = f32[61,16384]{1,0:T(8,128)} concatenate(f32[3,16384]{1,0:T(4,128)S(1)} %copy-done.1, f32[3,16384]{1,0:T(4,128)S(1)} %copy-done.3, f32[4,16384]{1,0:T(4,128)S(1)} %copy-done.2, f32[49,16384]{1,0:T(8,128)} %param.13, f32[1,16384]{1,0:T(1,128)S(1)} %bitcast.129, f32[1,16384]{1,0:T(1,128)S(1)} %bitcast.131), dimensions={0} | concatenate | bytes 7995392 | tf_op jit(solution)/shard_map/concatenate | solution.py:103
  165.8 6.9 %copy.40 = f32[16384,61]{1,0:T(8,128)} copy(f32[16384,61]{0,1:T(8,128)} %bitcast.126) | data formatting | bytes 7995392 | tf_op jit(solution)/shard_map/concatenate | solution.py:103
  172.7 44.3 %scatter_custom_fusion = f32[61,16384]{0,1:T(8,128)} fusion(s32[16384]{0:T(1024)} %get-tuple-element.78, f32[16384,61]{1,0:T(8,128)} %copy.40, f32[]{:T(128)} %constant.32.clone.1), kind=kCustom, calls=%fused_computation.3 | custom fusion | bytes 3998208 | tf_op jit(solution)/shard_map/scatter | solution.py:115
  217.0 7.7 %gather_fusion = f32[128,61,128]{1,2,0:T(8,128)} fusion(f32[61,128,128]{0,2,1:T(8,128)} %bitcast.125, s32[1024]{0:T(1024)S(1)} %pad_clamp_fusion), kind=kCustom, calls=%fused_computation | custom fusion | bytes 7995904 | tf_op jit(solution)/shard_map/gather | solution.py:124
  228.5 9.1 %all-to-all-start.3 = ((f32[32,1,3904]{2,1,0:T(1,128)}), f32[32,1,3904]{2,1,0:T(1,128)S(1)}, u32[]{:S(2)}, u32[]{:S(2)}) async-start(f32[32,1,3904]{2,1,0:T(1,128)} %reshape.640), calls=%async_computation.3 | async-start | bytes 1015808 | tf_op jit(solution)/shard_map/all_to_all | solution.py:135
  238.9 11.3 %all-to-all-done.3 = f32[32,1,3904]{2,1,0:T(1,128)S(1)} async-done(((f32[32,1,3904]{2,1,0:T(1,128)}), f32[32,1,3904]{2,1,0:T(1,128)S(1)}, u32[]{:S(2)}, u32[]{:S(2)}) %all-to-all-start.3) | async-done | bytes 499744 | tf_op jit(solution)/shard_map/all_to_all | solution.py:135
  254.2 4.5 %scatter_fusion = f32[61,128,16]{0,2,1:T(8,128)S(1)} fusion(f32[61,128,16]{0,2,1:T(8,128)S(1)} %broadcast_in_dim.44, s32[128]{0:T(128)S(1)} %fusion.4, f32[128,61,16]{1,2,0:T(8,128)S(1)} %bitcast.124), kind=kCustom, calls=%fused_computation.2 | custom fusion | bytes 1499648 | tf_op jit(solution)/shard_map/scatter | solution.py:142
  260.3 16.9 %all_to_all.31 = f32[32,1,1]{2,1,0:T(1,128)S(1)} all-to-all(f32[32,1,1]{2,1,0:T(1,128)S(1)} %broadcast_in_dim.51), channel_id=1, replica_groups=mesh['view'=8,'gauss'=32] {'gauss'}, dimensions={0} | all-to-all | bytes 256 | tf_op jit(solution)/shard_map/all_to_all | solution.py:11
  279.3 32.5 %all-gather.2.cloned.1.call-done = f32[61,128,128]{0,2,1:T(8,128)} async-done(((f32[61,128,16]{0,2,1:T(8,128)}), f32[61,128,128]{0,2,1:T(8,128)}) %all-gather.2.cloned.1.call-update) | async-done | bytes 3997712 | tf_op jit(solution)/shard_map/all_gather | solution.py:144
  311.8 6.8 %copy.42 = f32[61,16384]{1,0:T(8,128)} copy(f32[61,16384]{0,1:T(8,128)} %bitcast.127) | data formatting | bytes 7995392
  (82 shorter events, 44.5 us)
Async XLA Ops:
  7.2 101.4 %copy-start.3 = (f32[3,16384]{1,0:T(4,128)S(1)}, f32[3,16384]{1,0:T(4,128)}, u32[]{:S(2)}) copy-start(f32[3,16384]{1,0:T(4,128)} %param.11) | copy-start | bytes 589828
  7.2 102.1 %copy-start.4 = (f32[4,2,16384]{2,1,0:T(2,128)S(1)}, f32[4,2,16384]{2,1,0:T(2,128)}, u32[]{:S(2)}) copy-start(f32[4,2,16384]{2,1,0:T(2,128)} %param.14) | copy-start | bytes 1572868
  12.2 99.8 %all-to-all-start.1 = ((s32[32,1,1]{2,1,0:T(1,128)}), s32[32,1,1]{2,1,0:T(1,128)S(1)}, u32[]{:S(2)}, u32[]{:S(2)}) async-start(s32[32,1,1]{2,1,0:T(1,128)} %broadcast_in_dim.45), calls=%async_computation.1 | async-start | bytes 32768 | tf_op jit(solution)/shard_map/all_to_all | solution.py:11
  24.2 120.0 %copy-start.1 = (f32[3,16384]{1,0:T(4,128)S(1)}, f32[3,16384]{1,0:T(4,128)}, u32[]{:S(2)}) copy-start(f32[3,16384]{1,0:T(4,128)} %param.10) | copy-start | bytes 589828
  24.2 120.0 %copy-start.2 = (f32[4,16384]{1,0:T(4,128)S(1)}, f32[4,16384]{1,0:T(4,128)}, u32[]{:S(2)}) copy-start(f32[4,16384]{1,0:T(4,128)} %param.12) | copy-start | bytes 786436
  113.5 20.2 %all-to-all-start = ((f32[8,1,32768]{2,1,0:T(1,128)}), f32[8,1,32768]{2,1,0:T(1,128)S(1)}, u32[]{:S(2)}, u32[]{:S(2)}) async-start(f32[8,1,32768]{2,1,0:T(1,128)} %broadcast_in_dim.24), calls=%async_computation | async-start | bytes 2097152 | tf_op jit(solution)/shard_map/all_to_all | solution.py:11
  133.7 94.8 %all-to-all-start.2 = ((s32[1,32,4]{2,0,1:T(1,128)}), s32[1,32,4]{2,0,1:T(1,128)S(1)}, u32[]{:S(2)}, u32[]{:S(2)}) async-start(s32[1,32,4]{2,0,1:T(1,128)} %compare_select_fusion.1), calls=%async_computation.2 | async-start | bytes 32768 | tf_op jit(solution)/shard_map/all_to_all | solution.py:136
  228.5 21.8 %all-to-all-start.3 = ((f32[32,1,3904]{2,1,0:T(1,128)}), f32[32,1,3904]{2,1,0:T(1,128)S(1)}, u32[]{:S(2)}, u32[]{:S(2)}) async-start(f32[32,1,3904]{2,1,0:T(1,128)} %reshape.640), calls=%async_computation.3 | async-start | bytes 1015808 | tf_op jit(solution)/shard_map/all_to_all | solution.py:135
  237.6 74.3 %all-gather.2.cloned.1.call-start = ((), (), s32[]{:S(2)}) async-start(), calls=%async_computation.5 | async-start | bytes 9437184 | tf_op jit(solution)/shard_map/all_gather | solution.py:144
  258.8 1.0 copy-start
Sparse Core Ops, SparseCore 0:
  259.9 51.9 all-gather.1
where the time goes:
time: 329 us; the launch traced here: 327 us
  local copies, waits for them, and re-layouts  113 us (34%)
  other arithmetic  87.1 us (26%)
  waiting for transfers between devices  52.4 us (16%)
  starting transfers between devices  36.1 us (11%)
  between operations  21.3 us (6%)
  blocking collectives  16.9 us (5%)
    add x8, other arithmetic, view_stats(): first = [j00 * rot[0, j] + j02 * rot[2, j] for j in range(3)]  58.6 us
    scatter x1, local copies, waits for them, and re-layouts, body(): jnp.zeros((feat_rows, cap_blk * 128), jnp.float32).at[:, where_to]  44.3 us
    all_gather x1, waiting for transfers between devices, body(): placed = lax.all_gather(partial_place, 'view', axis=2, tiled=True)  32.5 us
    concatenate x2, local copies, waits for them, and re-layouts, body(): rows = jnp.concatenate([means, scales, quats, attrs, peak], axis=0)  28.5 us
    all_to_all x2, starting transfers between devices, copy_for_each(): lax.all_to_all(jnp.broadcast_to(x[None], (count, *x.shape)), axis, 0, 0,...  17.3 us
    all_to_all x1, blocking collectives, copy_for_each(): lax.all_to_all(jnp.broadcast_to(x[None], (count, *x.shape)), axis, 0, 0,...  16.9 us
    unnamed x15, local copies, waits for them, and re-layouts  11.7 us
    all_to_all x1, waiting for transfers between devices, body(): lax.all_to_all(portion, 'gauss', split_axis=1, concat_axis=1, tiled=True)  11.3 us
  transfers between devices with their start and end apart: 5, of which 3 were waited for; matrix products, arithmetic and copies ran while one was open for 54% of the time, Pallas kernels for 0%

commit v1 on v0

--- a/solution.py
+++ b/solution.py
@@ -1,9 +1,17 @@
+import functools
 import jax
 import jax.numpy as jnp
 from jax import lax
 from jax.sharding import PartitionSpec as P
 
 G_DEV = 16384
+
+
+def review_series(message, which_axis):
+    return jnp.concatenate(lax.all_gather(message, axis_name=which_axis), axis=2)
+
+
+resolve_frames = functools.partial(review_series, which_axis="view")
 
 
 def copy_for_each(x, axis):
@@ -141,7 +149,7 @@
         .at[:, slots_in.reshape(-1)]
         .set(arrived, mode="drop")
     )
-    placed = lax.all_gather(partial_place, "view", axis=2, tiled=True)
+    placed = resolve_frames(partial_place)
     clones = placed.reshape(feat_rows, cap_blk * 128)
     return (peak, clones, total)
 

time: 329 us -> 320 us (0.973)
  waiting for transfers between devices: 52.4 us -> 34.1 us
  local copies, waits for them, and re-layouts: 113 us -> 122 us
    all_gather x1, waiting for transfers between devices: 32.5 us -> 14 us  [review_series(): lax.all_gather(message, axis_name=which_axis)]
    reshape x1 -> x2, local copies, waits for them, and re-layouts: 1 us -> 10.3 us  [the longest x1 9.25 us: review_series(): jnp.concatenate(lax.all_gather(message, axis_name=which_axis), axis=2)]
    unnamed x15 -> x13, local copies, waits for them, and re-layouts: 11.7 us -> 10.7 us
  transfers between devices with their start and end apart: 5 -> 5, of which waited for: 3 -> 3; matrix products, arithmetic and copies ran while one was open for 54% -> 56% of each run, Pallas kernels for 0% -> 0%
where the time goes in v1:
time: 320 us; the launch traced here: 318 us
  local copies, waits for them, and re-layouts  122 us (38%)
  other arithmetic  87 us (27%)
  starting transfers between devices  36.1 us (11%)
  waiting for transfers between devices  34.1 us (11%)
  between operations  21.1 us (7%)
  blocking collectives  16.9 us (5%)
    add x8, other arithmetic, view_stats(): first = [j00 * rot[0, j] + j02 * rot[2, j] for j in range(3)]  58.4 us
    scatter x1, local copies, waits for them, and re-layouts, body(): jnp.zeros((feat_rows, cap_blk * 128), jnp.float32).at[:, where_to]  44.3 us
    concatenate x2, local copies, waits for them, and re-layouts, body(): rows = jnp.concatenate([means, scales, quats, attrs, peak], axis=0)  28.5 us
    all_to_all x2, starting transfers between devices, copy_for_each(): lax.all_to_all(jnp.broadcast_to(x[None], (count, *x.shape)), axis, 0, 0,...  17.3 us
    all_to_all x1, blocking collectives, copy_for_each(): lax.all_to_all(jnp.broadcast_to(x[None], (count, *x.shape)), axis, 0, 0,...  16.9 us
    all_gather x1, waiting for transfers between devices, review_series(): lax.all_gather(message, axis_name=which_axis)  14 us
    all_to_all x1, waiting for transfers between devices, body(): lax.all_to_all(portion, 'gauss', split_axis=1, concat_axis=1, tiled=True)  11.3 us
    unnamed x13, local copies, waits for them, and re-layouts  10.7 us
  transfers between devices with their start and end apart: 5, of which 3 were waited for; matrix products, arithmetic and copies ran while one was open for 56% of the time, Pallas kernels for 0%

profile of v1, /device:TPU:1, one launch (start us, length us, event | category | flops | bytes accessed | tf_op | source)
XLA Modules:
  0.0 317.6 jit_solution(1975091034847332997)
XLA Ops:
  12.3 12.0 %all-to-all-start.1 = ((s32[32,1,1]{2,1,0:T(1,128)}), s32[32,1,1]{2,1,0:T(1,128)S(1)}, u32[]{:S(2)}, u32[]{:S(2)}) async-start(s32[32,1,1]{2,1,0:T(1,128)} %broadcast_in_dim.45), calls=%async_computation.1 | async-start | bytes 32768 | tf_op jit(solution)/shard_map/all_to_all | solution.py:19
  33.8 7.2 %multiply_add_fusion.23 = (f32[1,16384]{1,0:T(1,128)S(1)}, f32[1,16384]{1,0:T(1,128)S(1)}, f32[1,16384]{1,0:T(1,128)S(1)}, f32[1,16384]{1,0:T(1,128)S(1)}) fusion(f32[]{:T(128)} %bitcast.13, f32[]{:T(128)} %bitcast.9, f32[]{:T(128)} %bitcast.16, f32[3,16384]{1,0:T(4,128)} %param.10, f32[]{:T(128)} %bitcast.15, f32[]{:T(128)} %bitcast.14, f32[]{:T(128)S(6)} %neg.16, ...), kind=kLoop, calls=%fused_computation.35 | loop fusion | flops 327680 | bytes 458792 | tf_op jit(solution)/shard_map/add | solution.py:80
  41.0 7.3 %multiply_add_fusion.22 = (f32[1,16384]{1,0:T(1,128)S(1)}, f32[1,16384]{1,0:T(1,128)S(1)}, f32[1,16384]{1,0:T(1,128)S(1)}, f32[1,16384]{1,0:T(1,128)S(1)}) fusion(f32[1,16384]{1,0:T(1,128)S(1)} %get-tuple-element.19, f32[1,16384]{1,0:T(1,128)S(1)} %get-tuple-element.20, f32[]{:T(128)} %bitcast.14, f32[]{:T(128)} %bitcast.10, f32[]{:T(128)} %bitcast.11, ...), kind=kLoop, calls=%fused_computation.34 | loop fusion | flops 294912 | bytes 655400 | tf_op jit(solution)/shard_map/add | solution.py:80
  52.2 7.3 %multiply_add_fusion.17 = (f32[1,16384]{1,0:T(1,128)S(1)}, f32[1,16384]{1,0:T(1,128)S(1)}, f32[1,16384]{1,0:T(1,128)S(1)}, f32[1,16384]{1,0:T(1,128)S(1)}) fusion(f32[]{:T(128)} %bitcast.39, f32[]{:T(128)} %bitcast.35, f32[]{:T(128)} %bitcast.42, f32[3,16384]{1,0:T(4,128)} %param.10, f32[]{:T(128)} %bitcast.41, f32[]{:T(128)} %bitcast.40, f32[]{:T(128)S(6)} %neg.17, ...), kind=kLoop, calls=%fused_computation.29 | loop fusion | flops 327680 | bytes 458792 | tf_op jit(solution)/shard_map/add | solution.py:80
  59.4 7.3 %multiply_add_fusion.16 = (f32[1,16384]{1,0:T(1,128)S(1)}, f32[1,16384]{1,0:T(1,128)S(1)}, f32[1,16384]{1,0:T(1,128)S(1)}, f32[1,16384]{1,0:T(1,128)S(1)}) fusion(f32[1,16384]{1,0:T(1,128)S(1)} %get-tuple-element.25, f32[1,16384]{1,0:T(1,128)S(1)} %get-tuple-element.26, f32[]{:T(128)} %bitcast.40, f32[]{:T(128)} %bitcast.36, f32[]{:T(128)} %bitcast.37, ...), kind=kLoop, calls=%fused_computation.28 | loop fusion | flops 294912 | bytes 655400 | tf_op jit(solution)/shard_map/add | solution.py:80
  70.7 7.4 %multiply_add_fusion.11 = (f32[1,16384]{1,0:T(1,128)S(1)}, f32[1,16384]{1,0:T(1,128)S(1)}, f32[1,16384]{1,0:T(1,128)S(1)}, f32[1,16384]{1,0:T(1,128)S(1)}) fusion(f32[]{:T(128)} %bitcast.58, f32[]{:T(128)} %bitcast.54, f32[]{:T(128)} %bitcast.61, f32[3,16384]{1,0:T(4,128)} %param.10, f32[]{:T(128)} %bitcast.60, f32[]{:T(128)} %bitcast.59, f32[]{:T(128)S(6)} %neg.18, ...), kind=kLoop, calls=%fused_computation.23 | loop fusion | flops 327680 | bytes 458792 | tf_op jit(solution)/shard_map/add | solution.py:80
  78.0 7.3 %multiply_add_fusion.10 = (f32[1,16384]{1,0:T(1,128)S(1)}, f32[1,16384]{1,0:T(1,128)S(1)}, f32[1,16384]{1,0:T(1,128)S(1)}, f32[1,16384]{1,0:T(1,128)S(1)}) fusion(f32[1,16384]{1,0:T(1,128)S(1)} %get-tuple-element.31, f32[1,16384]{1,0:T(1,128)S(1)} %get-tuple-element.32, f32[]{:T(128)} %bitcast.59, f32[]{:T(128)} %bitcast.55, f32[]{:T(128)} %bitcast.56, ...), kind=kLoop, calls=%fused_computation.22 | loop fusion | flops 294912 | bytes 655400 | tf_op jit(solution)/shard_map/add | solution.py:80
  89.2 7.4 %multiply_add_fusion.5 = (f32[1,16384]{1,0:T(1,128)S(1)}, f32[1,16384]{1,0:T(1,128)S(1)}, f32[1,16384]{1,0:T(1,128)S(1)}, f32[1,16384]{1,0:T(1,128)S(1)}) fusion(f32[]{:T(128)} %bitcast.77, f32[]{:T(128)} %bitcast.73, f32[]{:T(128)} %bitcast.80, f32[3,16384]{1,0:T(4,128)} %param.10, f32[]{:T(128)} %bitcast.79, f32[]{:T(128)} %bitcast.78, f32[]{:T(128)S(6)} %neg.19, ...), kind=kLoop, calls=%fused_computation.17 | loop fusion | flops 327680 | bytes 458792 | tf_op jit(solution)/shard_map/add | solution.py:80
  96.5 7.4 %multiply_add_fusion.4 = (f32[1,16384]{1,0:T(1,128)S(1)}, f32[1,16384]{1,0:T(1,128)S(1)}, f32[1,16384]{1,0:T(1,128)S(1)}, f32[1,16384]{1,0:T(1,128)S(1)}) fusion(f32[1,16384]{1,0:T(1,128)S(1)} %get-tuple-element.37, f32[1,16384]{1,0:T(1,128)S(1)} %get-tuple-element.38, f32[]{:T(128)} %bitcast.78, f32[]{:T(128)} %bitcast.74, f32[]{:T(128)} %bitcast.75, ...), kind=kLoop, calls=%fused_computation.16 | loop fusion | flops 294912 | bytes 655400 | tf_op jit(solution)/shard_map/add | solution.py:80
  103.9 2.6 multiply_add_fusion.1
  113.3 5.3 %all-to-all-start = ((f32[8,1,32768]{2,1,0:T(1,128)}), f32[8,1,32768]{2,1,0:T(1,128)S(1)}, u32[]{:S(2)}, u32[]{:S(2)}) async-start(f32[8,1,32768]{2,1,0:T(1,128)} %broadcast_in_dim.24), calls=%async_computation | async-start | bytes 2097152 | tf_op jit(solution)/shard_map/all_to_all | solution.py:19
  124.9 8.7 %all-to-all-done = f32[8,1,32768]{2,1,0:T(1,128)S(1)} async-done(((f32[8,1,32768]{2,1,0:T(1,128)}), f32[8,1,32768]{2,1,0:T(1,128)S(1)}, u32[]{:S(2)}, u32[]{:S(2)}) %all-to-all-start) | async-done | bytes 1048608 | tf_op jit(solution)/shard_map/all_to_all | solution.py:19
  133.5 9.7 %all-to-all-start.2 = ((s32[1,32,4]{2,0,1:T(1,128)}), s32[1,32,4]{2,0,1:T(1,128)S(1)}, u32[]{:S(2)}, u32[]{:S(2)}) async-start(s32[1,32,4]{2,0,1:T(1,128)} %compare_select_fusion.1), calls=%async_computation.2 | async-start | bytes 32768 | tf_op jit(solution)/shard_map/all_to_all | solution.py:144
  144.1 21.5 %concatenate.8 = f32[61,16384]{1,0:T(8,128)} concatenate(f32[3,16384]{1,0:T(4,128)S(1)} %copy-done, f32[3,16384]{1,0:T(4,128)S(1)} %copy-done.2, f32[4,16384]{1,0:T(4,128)S(1)} %copy-done.1, f32[49,16384]{1,0:T(8,128)} %param.13, f32[1,16384]{1,0:T(1,128)S(1)} %bitcast.133, f32[1,16384]{1,0:T(1,128)S(1)} %bitcast.135), dimensions={0} | concatenate | bytes 7995392 | tf_op jit(solution)/shard_map/concatenate | solution.py:111
  165.6 6.9 %copy.48 = f32[16384,61]{1,0:T(8,128)} copy(f32[16384,61]{0,1:T(8,128)} %bitcast.130) | data formatting | bytes 7995392 | tf_op jit(solution)/shard_map/concatenate | solution.py:111
  172.5 44.3 %scatter_custom_fusion = f32[61,16384]{0,1:T(8,128)} fusion(s32[16384]{0:T(1024)} %get-tuple-element.75, f32[16384,61]{1,0:T(8,128)} %copy.48, f32[]{:T(128)} %constant.32.clone.1), kind=kCustom, calls=%fused_computation.3 | custom fusion | bytes 3998208 | tf_op jit(solution)/shard_map/scatter | solution.py:123
  216.9 7.7 %gather_fusion = f32[128,61,128]{1,2,0:T(8,128)} fusion(f32[61,128,128]{0,2,1:T(8,128)} %bitcast.129, s32[1024]{0:T(1024)S(1)} %pad_clamp_fusion), kind=kCustom, calls=%fused_computation | custom fusion | bytes 7995904 | tf_op jit(solution)/shard_map/gather | solution.py:132
  228.3 9.1 %all-to-all-start.3 = ((f32[32,1,3904]{2,1,0:T(1,128)}), f32[32,1,3904]{2,1,0:T(1,128)S(1)}, u32[]{:S(2)}, u32[]{:S(2)}) async-start(f32[32,1,3904]{2,1,0:T(1,128)} %reshape.641), calls=%async_computation.3 | async-start | bytes 1015808 | tf_op jit(solution)/shard_map/all_to_all | solution.py:143
  238.8 11.3 %all-to-all-done.3 = f32[32,1,3904]{2,1,0:T(1,128)S(1)} async-done(((f32[32,1,3904]{2,1,0:T(1,128)}), f32[32,1,3904]{2,1,0:T(1,128)S(1)}, u32[]{:S(2)}, u32[]{:S(2)}) %all-to-all-start.3) | async-done | bytes 499744 | tf_op jit(solution)/shard_map/all_to_all | solution.py:143
  254.0 4.5 %scatter_fusion = f32[61,128,16]{0,2,1:T(8,128)S(1)} fusion(f32[61,128,16]{0,2,1:T(8,128)S(1)} %broadcast_in_dim.44, s32[128]{0:T(128)S(1)} %fusion.4, f32[128,61,16]{1,2,0:T(8,128)S(1)} %bitcast.128), kind=kCustom, calls=%fused_computation.2 | custom fusion | bytes 1499648 | tf_op jit(solution)/shard_map/scatter | solution.py:150
  260.6 16.9 %all_to_all.31 = f32[32,1,1]{2,1,0:T(1,128)S(1)} all-to-all(f32[32,1,1]{2,1,0:T(1,128)S(1)} %broadcast_in_dim.51), channel_id=1, replica_groups=mesh['view'=8,'gauss'=32] {'gauss'}, dimensions={0} | all-to-all | bytes 256 | tf_op jit(solution)/shard_map/all_to_all | solution.py:19
  279.5 14.0 %all-gather.3.cloned.1.call-done = f32[488,128,16]{1,2,0:T(8,128)} async-done(((f32[61,128,16]{1,2,0:T(8,128)}), f32[488,128,16]{1,2,0:T(8,128)}) %all-gather.3.cloned.1.call-update) | async-done | bytes 3997712 | tf_op jit(solution)/shard_map/all_gather | solution.py:11
  293.6 9.3 %copy.50 = f32[61,128,8,16]{0,3,2,1:T(8,128)} copy(f32[61,128,8,16]{1,3,0,2:T(8,128)} %bitcast.131) | data formatting | bytes 7995392 | tf_op jit(solution)/shard_map/reshape | solution.py:11
  302.8 6.8 %copy.52 = f32[61,16384]{1,0:T(8,128)} copy(f32[61,16384]{0,1:T(8,128)} %bitcast.127) | data formatting | bytes 7995392
  (82 shorter events, 47.4 us)
Async XLA Ops:
  7.2 101.2 %copy-start.2 = (f32[3,16384]{1,0:T(4,128)S(1)}, f32[3,16384]{1,0:T(4,128)}, u32[]{:S(2)}) copy-start(f32[3,16384]{1,0:T(4,128)} %param.11) | copy-start | bytes 589828
  7.2 102.0 %copy-start.3 = (f32[4,2,16384]{2,1,0:T(2,128)S(1)}, f32[4,2,16384]{2,1,0:T(2,128)}, u32[]{:S(2)}) copy-start(f32[4,2,16384]{2,1,0:T(2,128)} %param.14) | copy-start | bytes 1572868
  12.3 99.5 %all-to-all-start.1 = ((s32[32,1,1]{2,1,0:T(1,128)}), s32[32,1,1]{2,1,0:T(1,128)S(1)}, u32[]{:S(2)}, u32[]{:S(2)}) async-start(s32[32,1,1]{2,1,0:T(1,128)} %broadcast_in_dim.45), calls=%async_computation.1 | async-start | bytes 32768 | tf_op jit(solution)/shard_map/all_to_all | solution.py:19
  24.3 119.7 %copy-start = (f32[3,16384]{1,0:T(4,128)S(1)}, f32[3,16384]{1,0:T(4,128)}, u32[]{:S(2)}) copy-start(f32[3,16384]{1,0:T(4,128)} %param.10) | copy-start | bytes 589828
  24.4 119.7 %copy-start.1 = (f32[4,16384]{1,0:T(4,128)S(1)}, f32[4,16384]{1,0:T(4,128)}, u32[]{:S(2)}) copy-start(f32[4,16384]{1,0:T(4,128)} %param.12) | copy-start | bytes 786436
  113.3 20.2 %all-to-all-start = ((f32[8,1,32768]{2,1,0:T(1,128)}), f32[8,1,32768]{2,1,0:T(1,128)S(1)}, u32[]{:S(2)}, u32[]{:S(2)}) async-start(f32[8,1,32768]{2,1,0:T(1,128)} %broadcast_in_dim.24), calls=%async_computation | async-start | bytes 2097152 | tf_op jit(solution)/shard_map/all_to_all | solution.py:19
  133.5 94.8 %all-to-all-start.2 = ((s32[1,32,4]{2,0,1:T(1,128)}), s32[1,32,4]{2,0,1:T(1,128)S(1)}, u32[]{:S(2)}, u32[]{:S(2)}) async-start(s32[1,32,4]{2,0,1:T(1,128)} %compare_select_fusion.1), calls=%async_computation.2 | async-start | bytes 32768 | tf_op jit(solution)/shard_map/all_to_all | solution.py:144
  228.3 21.8 %all-to-all-start.3 = ((f32[32,1,3904]{2,1,0:T(1,128)}), f32[32,1,3904]{2,1,0:T(1,128)S(1)}, u32[]{:S(2)}, u32[]{:S(2)}) async-start(f32[32,1,3904]{2,1,0:T(1,128)} %reshape.641), calls=%async_computation.3 | async-start | bytes 1015808 | tf_op jit(solution)/shard_map/all_to_all | solution.py:143
  237.4 56.2 %all-gather.3.cloned.1.call-start = ((), (), s32[]{:S(2)}) async-start(), calls=%async_computation.5 | async-start | bytes 4497408 | tf_op jit(solution)/shard_map/all_gather | solution.py:11
Sparse Core Ops, SparseCore 0:
  260.0 33.4 all-gather.2
